TPU v7x, 8 devices: a whole 2x2x1 slice. The times are simulated.
8 devices in a mesh: replica: 2 (over z, y), data: 4 (over x, core).
Axes of the slice: x: 2, y: 2, z: 1, core: 2. Of those that a mesh axis runs over, the one named last changes fastest.
Arguments:
- grad_w1: float32 [2, 3, 128, 512], P('replica', None, 'data')
- grad_w2: float32 [2, 3, 512, 128], P('replica', None, 'data')
- master_w1: float32 [3, 128, 512], P(None, 'data')
- master_w2: float32 [3, 512, 128], P(None, 'data')
- moment1_w1: float32 [3, 128, 512], P(None, 'data')
- moment1_w2: float32 [3, 512, 128], P(None, 'data')
- moment2_w1: float32 [3, 128, 512], P(None, 'data')
- moment2_w2: float32 [3, 512, 128], P(None, 'data')
- tokens: bfloat16 [65536, 128], P(('replica', 'data'))
- targets: bfloat16 [65536, 128], P(('replica', 'data'))
Outputs:
- output 1: float32 [65536], P(('replica', 'data'))
- output 2: bfloat16 [3, 128, 512], replicated
- output 3: bfloat16 [3, 512, 128], replicated
- output 4: float32 [3, 128, 512], P(None, 'data')
- output 5: float32 [3, 512, 128], P(None, 'data')
- output 6: float32 [3, 128, 512], P(None, 'data')
- output 7: float32 [3, 512, 128], P(None, 'data')
- output 8: float32 [3, 128, 512], P(None, 'data')
- output 9: float32 [3, 512, 128], P(None, 'data')
All inputs are finite; a program needn't handle non-finite values.
Results may differ from a plain program's by a relative error of at most 0.00480666.
Values are sent between devices in bfloat16 or wider.
A program may use at most 1 GiB of HBM per device.

v0:
```python
import jax
import jax.numpy as jnp
from jax import lax
from jax.sharding import PartitionSpec as P, NamedSharding

ADAM_BETA1 = 0.9
ADAM_BETA2 = 0.95
ADAM_EPS = 1e-8
WEIGHT_DECAY = 0.1
STEP = 2
NORM_EPS = 1e-6
LR_COEF = 0.2


def adam_shard(grad_mean, master, moment1, moment2, learn_rate):
    new_m = ADAM_BETA1 * moment1 + (1.0 - ADAM_BETA1) * grad_mean
    new_v = ADAM_BETA2 * moment2 + (1.0 - ADAM_BETA2) * grad_mean * grad_mean
    corr_m = 1.0 - ADAM_BETA1 ** STEP
    corr_v = 1.0 - ADAM_BETA2 ** STEP
    step_dir = (new_m / corr_m) / (jnp.sqrt(new_v / corr_v) + ADAM_EPS)
    new_w = master - learn_rate * (step_dir + WEIGHT_DECAY * master)
    return new_w, new_m, new_v


def rms_norm(hidden):
    hidden_f32 = hidden.astype(jnp.float32)
    inv_rms = lax.rsqrt(jnp.mean(hidden_f32 * hidden_f32, axis=-1, keepdims=True) + NORM_EPS)
    return (hidden_f32 * inv_rms).astype(jnp.bfloat16)


def block_forward(hidden, w_up, w_down):
    normed = rms_norm(hidden)
    up_act = jnp.dot(normed, w_up, preferred_element_type=jnp.float32).astype(jnp.bfloat16)
    gelu_act = jax.nn.gelu(up_act.astype(jnp.float32), approximate=True).astype(jnp.bfloat16)
    down_out = jnp.dot(gelu_act, w_down, preferred_element_type=jnp.float32)
    return (hidden.astype(jnp.float32) + down_out).astype(jnp.bfloat16)


def solution(mesh):
    replicas = mesh.shape['replica']
    grad_spec = P('replica', None, 'data', None)
    shard_spec = P(None, 'data', None)
    row_spec = P(('replica', 'data'), None)
    loss_spec = P(('replica', 'data'))
    full_spec = P()

    def local_step(grad_w1, grad_w2, master_w1, master_w2, moment1_w1, moment1_w2, moment2_w1, moment2_w2, tokens, targets):
        learn_rate = LR_COEF * tokens.shape[1] ** -0.5
        grad_mean1 = lax.psum(grad_w1[0], 'replica') / replicas
        grad_mean2 = lax.psum(grad_w2[0], 'replica') / replicas
        new_w1, new_m1, new_v1 = adam_shard(grad_mean1, master_w1, moment1_w1, moment2_w1, learn_rate)
        new_w2, new_m2, new_v2 = adam_shard(grad_mean2, master_w2, moment1_w2, moment2_w2, learn_rate)
        half_w1 = new_w1.astype(jnp.bfloat16)
        half_w2 = new_w2.astype(jnp.bfloat16)
        hidden = tokens
        gathered_w1 = []
        gathered_w2 = []
        for layer_idx in range(half_w1.shape[0]):
            layer_w1 = lax.all_gather(half_w1[layer_idx], 'data', axis=0, tiled=True)
            layer_w2 = lax.all_gather(half_w2[layer_idx], 'data', axis=0, tiled=True)
            hidden = block_forward(hidden, layer_w1, layer_w2)
            gathered_w1.append(layer_w1)
            gathered_w2.append(layer_w2)
        row_diff = hidden.astype(jnp.float32) - targets.astype(jnp.float32)
        row_loss = jnp.mean(row_diff * row_diff, axis=-1)
        return (row_loss, jnp.stack(gathered_w1), jnp.stack(gathered_w2), new_w1, new_w2, new_m1, new_m2, new_v1, new_v2)

    return jax.shard_map(
        local_step,
        mesh=mesh,
        in_specs=(grad_spec, grad_spec, shard_spec, shard_spec, shard_spec, shard_spec, shard_spec, shard_spec, row_spec, row_spec),
        out_specs=(loss_spec, full_spec, full_spec, shard_spec, shard_spec, shard_spec, shard_spec, shard_spec, shard_spec),
        check_vma=False,
    )
```

profile of v0, /device:TPU:0, one launch (start us, length us, event | category | flops | bytes accessed | tf_op | source)
XLA Modules:
  0.0 123.8 jit_solution(14217900118062444266)
XLA Ops:
  7.2 0.0 all-reduce.3.cloned.1.call-start
  7.2 0.7 all-reduce.3.cloned.1.call-update
  7.9 2.9 %copy.19 = bf16[8192,128]{0,1:T(8,128)(2,1)S(1)} copy(bf16[8192,128]{1,0:T(8,128)(2,1)} %param.18) | data formatting | bytes 4194304 | tf_op args[8]
  10.8 0.0 copy-start.1
  10.8 0.0 copy-start.2
  10.8 0.0 copy-start.3
  10.9 0.0 copy-start.6
  10.9 4.2 %copy.20 = bf16[8192,128]{0,1:T(8,128)(2,1)} copy(bf16[8192,128]{1,0:T(8,128)(2,1)} %param.19) | data formatting | bytes 4194304 | tf_op args[9]
  15.1 0.5 fusion.38
  15.6 17.6 %all-reduce.3.cloned.1.call-done = (f32[3,128,128]{2,1,0:T(8,128)}, f32[3,32,512]{2,1,0:T(8,128)}) async-done(((f32[3,128,128]{2,1,0:T(8,128)}, f32[3,32,512]{2,1,0:T(8,128)}), (f32[3,128,128]{2,1,0:T(8,128)}, f32[3,32,512]{2,1,0:T(8,128)})) %all-reduce.3.cloned.1.call-update) | async-done | bytes 393232 | tf_op jit(solution)/shard_map/psum | solution.py:50
  33.2 1.8 %fusion.72 = (bf16[3,32,512]{2,1,0:T(8,128)(2,1)S(1)}, f32[3,32,512]{2,1,0:T(8,128)}, f32[3,32,512]{2,1,0:T(8,128)}, f32[3,32,512]{2,1,0:T(8,128)}) fusion(f32[3,32,512]{2,1,0:T(8,128)S(1)} %copy-done.1, f32[3,32,512]{2,1,0:T(8,128)} %get-tuple-element.10, f32[3,32,512]{2,1,0:T(8,128)S(1)} %copy-done.2, f32[3,32,512]{2,1,0:T(8,128)S(1)} %copy-done.3), kind=kLoop, calls=%fused_computation.95 | loop fusion | flops 835584 | bytes 1474560 | tf_op jit(solution)/shard_map/convert_element_type | solution.py:53
  35.0 8.4 %all-gather = bf16[1,128,512]{2,1,0:T(8,128)(2,1)S(1)} all-gather(bf16[1,32,512]{2,1,0:T(8,128)(2,1)S(1)} %get-tuple-element.21), channel_id=2, replica_groups=mesh['replica'=2,'data'=4] {'data'}, dimensions={1}, use_global_device_ids=true | all-gather | bytes 163840 | tf_op jit(solution)/shard_map/all_gather | solution.py:59
  43.5 1.8 %fusion.73 = (bf16[3,128,128]{2,1,0:T(8,128)(2,1)S(1)}, f32[3,128,128]{2,1,0:T(8,128)}, f32[3,128,128]{2,1,0:T(8,128)}, f32[3,128,128]{2,1,0:T(8,128)}) fusion(f32[3,128,128]{2,1,0:T(8,128)S(1)} %copy-done.4, f32[3,128,128]{2,1,0:T(8,128)} %get-tuple-element.9, f32[3,128,128]{2,1,0:T(8,128)S(1)} %copy-done.5, f32[3,128,128]{2,1,0:T(8,128)S(1)} %copy-done.6), kind=kLoop, calls=%fused_computation.96 | loop fusion | flops 835584 | bytes 1474560 | tf_op jit(solution)/shard_map/convert_element_type | solution.py:54
  45.3 7.5 %all-gather.1 = bf16[1,512,128]{2,1,0:T(8,128)(2,1)S(1)} all-gather(bf16[1,128,128]{2,1,0:T(8,128)(2,1)S(1)} %get-tuple-element.24), channel_id=3, replica_groups=mesh['replica'=2,'data'=4] {'data'}, dimensions={1}, use_global_device_ids=true | all-gather | bytes 163840 | tf_op jit(solution)/shard_map/all_gather | solution.py:60
  52.8 9.2 %multiply_reduce_fusion.1 = (f32[8192]{0:T(1024)S(1)}, f32[8192,128]{0,1:T(8,128)}) fusion(bf16[1,512,128]{2,1,0:T(8,128)(2,1)S(1)} %all-gather.1, bf16[8192,128]{0,1:T(8,128)(2,1)S(1)} %copy.19, f32[8192]{0:T(1024)S(1)} %add_rsqrt_fusion.2, bf16[1,128,512]{2,1,0:T(8,128)(2,1)S(1)} %all-gather), kind=kOutput, calls=%fused_computation.60 | convolution fusion | flops 2203049984 | bytes 6619136 | tf_op jit(solution)/shard_map/dot_general | solution.py:35
  62.0 8.4 %all-gather.2 = bf16[1,128,512]{2,1,0:T(8,128)(2,1)S(1)} all-gather(bf16[1,32,512]{2,1,0:T(8,128)(2,1)S(1)} %get-tuple-element.20), channel_id=4, replica_groups=mesh['replica'=2,'data'=4] {'data'}, dimensions={1}, use_global_device_ids=true | all-gather | bytes 163840 | tf_op jit(solution)/shard_map/all_gather | solution.py:59
  70.4 7.5 %all-gather.3 = bf16[1,512,128]{2,1,0:T(8,128)(2,1)S(1)} all-gather(bf16[1,128,128]{2,1,0:T(8,128)(2,1)S(1)} %get-tuple-element.23), channel_id=5, replica_groups=mesh['replica'=2,'data'=4] {'data'}, dimensions={1}, use_global_device_ids=true | all-gather | bytes 163840 | tf_op jit(solution)/shard_map/all_gather | solution.py:60
  77.9 11.0 %multiply_reduce_fusion = (f32[8192]{0:T(1024)S(1)}, f32[8192,128]{0,1:T(8,128)}) fusion(f32[8192,128]{0,1:T(8,128)} %get-tuple-element.26, bf16[1,512,128]{2,1,0:T(8,128)(2,1)S(1)} %all-gather.3, f32[8192]{0:T(1024)S(1)} %add_rsqrt_fusion.1, bf16[1,128,512]{2,1,0:T(8,128)(2,1)S(1)} %all-gather.2), kind=kOutput, calls=%fused_computation.58 | convolution fusion | flops 2200952832 | bytes 8716288 | tf_op jit(solution)/shard_map/dot_general | solution.py:35
  88.9 8.4 %all-gather.4 = bf16[1,128,512]{2,1,0:T(8,128)(2,1)S(1)} all-gather(bf16[1,32,512]{2,1,0:T(8,128)(2,1)S(1)} %get-tuple-element.19), channel_id=6, replica_groups=mesh['replica'=2,'data'=4] {'data'}, dimensions={1}, use_global_device_ids=true | all-gather | bytes 163840 | tf_op jit(solution)/shard_map/all_gather | solution.py:59
  97.3 7.7 %all-gather.5 = bf16[1,512,128]{2,1,0:T(8,128)(2,1)S(1)} all-gather(bf16[1,128,128]{2,1,0:T(8,128)(2,1)S(1)} %get-tuple-element.22), channel_id=7, replica_groups=mesh['replica'=2,'data'=4] {'data'}, dimensions={1}, use_global_device_ids=true | all-gather | bytes 163840 | tf_op jit(solution)/shard_map/all_gather | solution.py:60
  105.0 0.8 pad_maximum_fusion
  105.8 0.8 pad_maximum_fusion.1
  106.6 9.8 %fusion.48 = f32[8192]{0:T(1024)S(1)} fusion(bf16[8192,128]{0,1:T(8,128)(2,1)S(1)} %copy-done, f32[8192,128]{0,1:T(8,128)} %get-tuple-element.28, f32[8192]{0:T(1024)S(1)} %add_rsqrt_fusion, bf16[1,512,128]{2,1,0:T(8,128)(2,1)S(1)} %all-gather.5, bf16[1,128,512]{2,1,0:T(8,128)(2,1)S(1)} %all-gather.4), kind=kOutput, calls=%fused_computation.64 | convolution fusion | flops 2203049984 | bytes 6619136 | tf_op jit(solution)/shard_map/dot_general | solution.py:35
  116.4 0.6 broadcast_multiply_fusion
  (15 shorter events, 0.1 us)
Async XLA Ops:
  7.2 26.0 %all-reduce.3.cloned.1.call-start = ((), (), s32[]{:S(2)}) async-start(), calls=%async_computation | async-start | bytes 786432 | tf_op jit(solution)/shard_map/psum | solution.py:50
  10.8 22.4 %copy-start.1 = (f32[3,32,512]{2,1,0:T(8,128)S(1)}, f32[3,32,512]{2,1,0:T(8,128)}, u32[]{:S(2)}) copy-start(f32[3,32,512]{2,1,0:T(8,128)} %param.12) | copy-start | bytes 589828
  10.8 22.4 %copy-start.2 = (f32[3,32,512]{2,1,0:T(8,128)S(1)}, f32[3,32,512]{2,1,0:T(8,128)}, u32[]{:S(2)}) copy-start(f32[3,32,512]{2,1,0:T(8,128)} %param.14) | copy-start | bytes 589828
  10.8 22.4 %copy-start.3 = (f32[3,32,512]{2,1,0:T(8,128)S(1)}, f32[3,32,512]{2,1,0:T(8,128)}, u32[]{:S(2)}) copy-start(f32[3,32,512]{2,1,0:T(8,128)} %param.16) | copy-start | bytes 589828
  10.9 32.6 %copy-start.4 = (f32[3,128,128]{2,1,0:T(8,128)S(1)}, f32[3,128,128]{2,1,0:T(8,128)}, u32[]{:S(2)}) copy-start(f32[3,128,128]{2,1,0:T(8,128)} %param.13) | copy-start | bytes 589828
  10.9 32.6 %copy-start.5 = (f32[3,128,128]{2,1,0:T(8,128)S(1)}, f32[3,128,128]{2,1,0:T(8,128)}, u32[]{:S(2)}) copy-start(f32[3,128,128]{2,1,0:T(8,128)} %param.15) | copy-start | bytes 589828
  10.9 32.6 %copy-start.6 = (f32[3,128,128]{2,1,0:T(8,128)S(1)}, f32[3,128,128]{2,1,0:T(8,128)}, u32[]{:S(2)}) copy-start(f32[3,128,128]{2,1,0:T(8,128)} %param.17) | copy-start | bytes 589828
  77.9 28.7 %copy-start = (bf16[8192,128]{0,1:T(8,128)(2,1)S(1)}, bf16[8192,128]{0,1:T(8,128)(2,1)}, u32[]{:S(2)}) copy-start(bf16[8192,128]{0,1:T(8,128)(2,1)} %copy.20) | copy-start | bytes 6291460
Sparse Core Ops, SparseCore 0:
  10.3 22.8 all-reduce.2
where the time goes:
time: 124 us
  blocking collectives  47.9 us (39%)
  matrix products  29.9 us (24%)
  waiting for transfers between devices  18.3 us (15%)
  between operations  14.2 us (11%)
  local copies, waits for them, and re-layouts  7.16 us (6%)
  other arithmetic  6.36 us (5%)
    dot_general x3, matrix products, block_forward(): down_out = jnp.dot(gelu_act, w_down, preferred_element_type=jnp.float32)  29.9 us
    all_gather x3, blocking collectives, local_step(): layer_w1 = lax.all_gather(half_w1[layer_idx], 'data', axis=0, tiled=True)  25.2 us
    all_gather x3, blocking collectives, local_step(): layer_w2 = lax.all_gather(half_w2[layer_idx], 'data', axis=0, tiled=True)  22.7 us
    psum x1, waiting for transfers between devices, local_step(): grad_mean2 = lax.psum(grad_w2[0], 'replica') / replicas  17.6 us
    unnamed x16, local copies, waits for them, and re-layouts  7.14 us
  transfers between devices with their start and end apart: 1, of which 1 were waited for; matrix products, arithmetic and copies ran while one was open for 6% of the time, Pallas kernels for 0%

commit v1 on v0

v1 whole, which is shorter than its diff:
```python
import jax
import jax.numpy as jnp
from jax import lax
from jax.experimental import pallas as pl
from jax.experimental.pallas import tpu as pltpu
from jax.sharding import PartitionSpec as P

ADAM_BETA1 = 0.9
ADAM_BETA2 = 0.95
ADAM_EPS = 1e-8
WEIGHT_DECAY = 0.1
STEP = 2
NORM_EPS = 1e-6
LR_COEF = 0.2
GELU_A = 2.0 * (2.0 / jnp.pi) ** 0.5
GELU_B = 8.0 * (2.0 / jnp.pi) ** 0.5 * 0.044715

F32 = jnp.float32
BF16 = jnp.bfloat16
MESH = pl.DeviceIdType.MESH
ROWS = 2048
VMEM_LIMIT = 60 * 1024 * 1024


def adam_shard(grad_mean, master, moment1, moment2, learn_rate):
    new_m = ADAM_BETA1 * moment1 + (1.0 - ADAM_BETA1) * grad_mean
    new_v = ADAM_BETA2 * moment2 + (1.0 - ADAM_BETA2) * grad_mean * grad_mean
    corr_m = 1.0 - ADAM_BETA1 ** STEP
    corr_v = 1.0 - ADAM_BETA2 ** STEP
    step_dir = (new_m / corr_m) / (jnp.sqrt(new_v / corr_v) + ADAM_EPS)
    new_w = master - learn_rate * (step_dir + WEIGHT_DECAY * master)
    return new_w, new_m, new_v


def rms_norm(hidden):
    inv_rms = lax.rsqrt(jnp.mean(hidden * hidden, axis=-1, keepdims=True) + NORM_EPS)
    return (hidden * inv_rms).astype(BF16)


def mlp(normed, hidden, half_up, down):
    half = jnp.dot(normed.astype(F32), half_up, preferred_element_type=F32).astype(BF16).astype(F32)
    act = half * jnp.tanh(half * (GELU_B * (half * half) + GELU_A)) + half
    act = act.astype(BF16).astype(F32)
    return (hidden + jnp.dot(act, down, preferred_element_type=F32)).astype(BF16)


def step_kernel(learn_rate, replicas,
                g1, g2, w1, w2, m1, m2, v1, v2, x,
                h_out, fw1_out, fw2_out, nw1, nw2, nm1, nm2, nv1, nv2,
                g1v, g2v, r1v, r2v, s1, s2, fw1, fw2, xv, nv, up, down,
                sem_g, sem_s, sem_x, sem_out, send_g, recv_g, send_w, recv_w):
    rep, dat = lax.axis_index('replica'), lax.axis_index('data')
    layers = g1.shape[1]
    rows1, rows2 = w1.shape[1], w2.shape[1]
    n_rows = x.shape[0]
    tiles = n_rows // ROWS
    twin = {'replica': 1 - rep}
    peers = [{'data': d} for d in (dat + 1 - 2 * lax.rem(dat, 2), lax.rem(dat + 2, 4), 3 - dat)]

    gcopies = [[pltpu.make_async_copy(g.at[0, l], gv.at[l], sem_g.at[l, k])
                for k, (g, gv) in enumerate(((g1, g1v), (g2, g2v)))] for l in range(layers)]
    for pair in gcopies:
        for c in pair:
            c.start()
    xcopies = [pltpu.make_async_copy(x.at[pl.ds(t * ROWS, ROWS)], xv.at[pl.ds(t * ROWS, ROWS)], sem_x.at[t])
               for t in range(tiles)]
    for c in xcopies:
        c.start()
    scopies = [pltpu.make_async_copy(src, dst.at[i], sem_s.at[k, i])
               for k, (srcs, dst) in enumerate((((w1, m1, v1), s1), ((w2, m2, v2), s2)))
               for i, src in enumerate(srcs)]
    for c in scopies:
        c.start()

    barrier = pltpu.get_barrier_semaphore()
    for dev in [twin] + peers:
        pl.semaphore_signal(barrier, inc=1, device_id=dev, device_id_type=MESH)
    pl.semaphore_wait(barrier, 4)

    gsends = []
    for l in range(layers):
        row = []
        for k, (gv, rv) in enumerate(((g1v, r1v), (g2v, r2v))):
            gcopies[l][k].wait()
            c = pltpu.make_async_remote_copy(
                src_ref=gv.at[l], dst_ref=rv.at[l], send_sem=send_g.at[l, k], recv_sem=recv_g.at[l, k],
                device_id=twin, device_id_type=MESH)
            c.start()
            row.append(c)
        gsends.append(row)

    for t in range(tiles):
        xcopies[t].wait()
        sl = pl.ds(t * ROWS, ROWS)
        nv[sl] = rms_norm(xv[sl].astype(F32))
    for c in scopies:
        c.wait()

    wsends = {}

    def update(l, k):
        gv, rv, s, fw, rows = ((g1v, r1v, s1, fw1, rows1), (g2v, r2v, s2, fw2, rows2))[k]
        gsends[l][k].wait_recv()
        mean = (gv[l] + rv[l]) / replicas
        new_w, new_m, new_v = adam_shard(mean, s[0, l], s[1, l], s[2, l], learn_rate)
        s[0, l], s[1, l], s[2, l] = new_w, new_m, new_v
        mine = pl.ds(pl.multiple_of(dat * rows, rows), rows)
        fw[l, mine] = new_w.astype(BF16)
        out = []
        for j, dev in enumerate(peers):
            c = pltpu.make_async_remote_copy(
                src_ref=fw.at[l, mine], dst_ref=fw.at[l, mine], send_sem=send_w.at[l, k, j],
                recv_sem=recv_w.at[l, k, j], device_id=dev, device_id_type=MESH)
            c.start()
            out.append(c)
        wsends[l, k] = out

    def arrived(l, k):
        for c in wsends[l, k]:
            c.wait_recv()

    update(0, 0)
    update(0, 1)
    update(1, 0)
    arrived(0, 0)
    arrived(0, 1)
    up[...] = fw1[0].astype(F32) * 0.5
    down[...] = fw2[0].astype(F32)
    hcopies = []
    later = {0: ((1, 1),), 1: ((2, 0), (2, 1))}
    for t in range(tiles):
        sl = pl.ds(t * ROWS, ROWS)
        xv[sl] = mlp(nv[sl], xv[sl].astype(F32), up[...], down[...])
        c = pltpu.make_async_copy(xv.at[sl], h_out.at[sl], sem_x.at[t])
        c.start()
        hcopies.append(c)
        for l, k in later.get(t, ()):
            update(l, k)
    outs = [pltpu.make_async_copy(s.at[i], dst, sem_s.at[k, i])
            for k, (s, dsts) in enumerate(((s1, (nw1, nm1, nv1)), (s2, (nw2, nm2, nv2))))
            for i, dst in enumerate(dsts)]
    for c in outs:
        c.start()
    for l in range(1, layers):
        for k in range(2):
            arrived(l, k)
    outs += [pltpu.make_async_copy(fw1, fw1_out, sem_out.at[0]), pltpu.make_async_copy(fw2, fw2_out, sem_out.at[1])]
    for c in outs[-2:]:
        c.start()
    for l in range(layers):
        for k in range(2):
            gsends[l][k].wait_send()
            for c in wsends[l, k]:
                c.wait_send()
    for c in outs + hcopies:
        c.wait()


def tail_kernel(h_in, y, fw1_in, fw2_in, nw1, nw2, nm1, nm2, nv1, nv2,
                loss, fw1_out, fw2_out, ow1, ow2, om1, om2, ov1, ov2,
                hv, yv, fw1, fw2, s1, s2, up, down, sem_h, sem_y, sem_f, sem_s):
    layers = fw1.shape[0]
    tiles = hv.shape[0] // ROWS
    fin = [pltpu.make_async_copy(fw1_in, fw1, sem_f.at[0]), pltpu.make_async_copy(fw2_in, fw2, sem_f.at[1])]
    for c in fin:
        c.start()
    hcs, ycs = [], []
    for t in range(tiles):
        sl = pl.ds(t * ROWS, ROWS)
        hcs.append(pltpu.make_async_copy(h_in.at[sl], hv.at[sl], sem_h.at[t]))
        ycs.append(pltpu.make_async_copy(y.at[sl], yv.at[sl], sem_y.at[t]))
        hcs[-1].start()
        ycs[-1].start()
    sin = [pltpu.make_async_copy(src, dst.at[i], sem_s.at[k, i])
           for k, (srcs, dst) in enumerate((((nw1, nm1, nv1), s1), ((nw2, nm2, nv2), s2)))
           for i, src in enumerate(srcs)]
    for c in sin:
        c.start()
    for c in fin:
        c.wait()
    fout = [pltpu.make_async_copy(fw1, fw1_out, sem_f.at[0]), pltpu.make_async_copy(fw2, fw2_out, sem_f.at[1])]
    for c in fout:
        c.start()
    for l in range(1, layers):
        up[l - 1] = fw1[l].astype(F32) * 0.5
        down[l - 1] = fw2[l].astype(F32)
    for c in sin:
        c.wait()
    sout = [pltpu.make_async_copy(s.at[i], dst, sem_s.at[k, i])
            for k, (s, dsts) in enumerate(((s1, (ow1, om1, ov1)), (s2, (ow2, om2, ov2))))
            for i, dst in enumerate(dsts)]
    for c in sout:
        c.start()

    def tile(t, _):
        sl = pl.ds(pl.multiple_of(t * ROWS, ROWS), ROWS)
        pltpu.make_async_copy(h_in.at[sl], hv.at[sl], sem_h.at[t]).wait()
        hidden = hv[sl]
        for l in range(layers - 1):
            wide = hidden.astype(F32)
            hidden = mlp(rms_norm(wide), wide, up[l], down[l])
        pltpu.make_async_copy(y.at[sl], yv.at[sl], sem_y.at[t]).wait()
        diff = hidden.astype(F32) - yv[sl].astype(F32)
        loss[:, sl] = jnp.mean(diff * diff, axis=-1, keepdims=True).reshape(1, ROWS)
        return 0

    lax.fori_loop(0, tiles, tile, 0)
    for c in fout + sout:
        c.wait()


def solution(mesh):
    replicas = mesh.shape['replica']
    grad_spec = P('replica', None, 'data', None)
    shard_spec = P(None, 'data', None)
    row_spec = P(('replica', 'data'), None)
    loss_spec = P(('replica', 'data'))
    full_spec = P()

    def local_step(g1, g2, w1, w2, m1, m2, v1, v2, tokens, targets):
        learn_rate = LR_COEF * tokens.shape[1] ** -0.5
        n_rows, width = tokens.shape
        layers, rows1, hid = w1.shape
        rows2 = w2.shape[1]
        any_ = pl.BlockSpec(memory_space=pl.ANY)
        full1 = (layers, width, hid)
        full2 = (layers, hid, width)
        tiles = n_rows // ROWS
        sh = jax.ShapeDtypeStruct
        dma = pltpu.SemaphoreType.DMA
        state = [sh(w1.shape, F32), sh(w2.shape, F32)] * 3
        step = pl.pallas_call(
            lambda *refs: step_kernel(learn_rate, replicas, *refs),
            out_shape=[sh((n_rows, width), BF16), sh(full1, BF16), sh(full2, BF16)] + state,
            in_specs=[any_] * 9,
            out_specs=[any_] * 9,
            scratch_shapes=[
                pltpu.VMEM(w1.shape, F32), pltpu.VMEM(w2.shape, F32),
                pltpu.VMEM(w1.shape, F32), pltpu.VMEM(w2.shape, F32),
                pltpu.VMEM((3,) + w1.shape, F32), pltpu.VMEM((3,) + w2.shape, F32),
                pltpu.VMEM(full1, BF16), pltpu.VMEM(full2, BF16),
                pltpu.VMEM((n_rows, width), BF16), pltpu.VMEM((n_rows, width), BF16),
                pltpu.VMEM((width, hid), F32), pltpu.VMEM((hid, width), F32),
                dma((layers, 2)), dma((2, 3)), dma((tiles,)), dma((2,)),
                dma((layers, 2)), dma((layers, 2)), dma((layers, 2, 3)), dma((layers, 2, 3)),
            ],
            compiler_params=pltpu.CompilerParams(
                collective_id=0, has_side_effects=True, vmem_limit_bytes=VMEM_LIMIT),
            name='step',
        )
        mid = step(g1, g2, w1, w2, m1, m2, v1, v2, tokens)
        tail = pl.pallas_call(
            tail_kernel,
            out_shape=[sh((1, n_rows), F32), sh(full1, BF16), sh(full2, BF16)] + state,
            in_specs=[any_] * 10,
            out_specs=[pl.BlockSpec(memory_space=pltpu.VMEM)] + [any_] * 8,
            scratch_shapes=[
                pltpu.VMEM((n_rows, width), BF16), pltpu.VMEM((n_rows, width), BF16),
                pltpu.VMEM(full1, BF16), pltpu.VMEM(full2, BF16),
                pltpu.VMEM((3,) + w1.shape, F32), pltpu.VMEM((3,) + w2.shape, F32),
                pltpu.VMEM((layers - 1, width, hid), F32), pltpu.VMEM((layers - 1, hid, width), F32),
                dma((tiles,)), dma((tiles,)), dma((2,)), dma((2, 3)),
            ],
            compiler_params=pltpu.CompilerParams(vmem_limit_bytes=VMEM_LIMIT),
            name='tail',
        )
        outs = tail(mid[0], targets, *mid[1:])
        return (outs[0].reshape(n_rows),) + tuple(outs[1:])

    return jax.shard_map(
        local_step,
        mesh=mesh,
        in_specs=(grad_spec, grad_spec, shard_spec, shard_spec, shard_spec, shard_spec, shard_spec, shard_spec, row_spec, row_spec),
        out_specs=(loss_spec, full_spec, full_spec, shard_spec, shard_spec, shard_spec, shard_spec, shard_spec, shard_spec),
        check_vma=False,
    )
```

time: 124 us -> 43.6 us (0.35)
  blocking collectives: 47.9 us -> 0 us
  Pallas kernels: 0 us -> 42.7 us
  matrix products: 29.9 us -> 0 us
  waiting for transfers between devices: 18.3 us -> 0 us
  between operations: 14.2 us -> 0.81 us
  local copies, waits for them, and re-layouts: 7.16 us -> 0 us
  other arithmetic: 6.36 us -> 0 us
    all_gather x6 -> x0, blocking collectives: 47.9 us -> none  [the longest x3 25.2 us: local_step(): layer_w1 = lax.all_gather(half_w1[layer_idx], 'data', axis=0, tiled=True)]
    pallas_call x0 -> x2, Pallas kernels: none -> 42.7 us  [the longest x1 23.5 us: local_step(): mid = step(g1, g2, w1, w2, m1, m2, v1, v2, tokens)]
    dot_general x3 -> x0, matrix products: 29.9 us -> none  [block_forward(): down_out = jnp.dot(gelu_act, w_down, preferred_element_type=jnp.float32)]
    psum x1 -> x0, waiting for transfers between devices: 17.6 us -> none  [local_step(): grad_mean2 = lax.psum(grad_w2[0], 'replica') / replicas]
    unnamed x16 -> x0, local copies, waits for them, and re-layouts: 7.14 us -> none
    convert_element_type x2 -> x0, other arithmetic: 3.66 us -> none  [the longest x1 1.83 us: local_step(): half_w2 = new_w2.astype(jnp.bfloat16)]
    another operation x2 -> x0, other arithmetic: 1.58 us -> none  [the longest x1 0.79 us: local_step(): jnp.stack(gathered_w1)]
  transfers between devices with their start and end apart: 1 -> 0, of which waited for: 1 -> 0; matrix products, arithmetic and copies ran while one was open for 6% -> 0% of each run, Pallas kernels for 0% -> 0%
where the time goes in v1:
time: 43.6 us; the launch traced here: 43.5 us
  Pallas kernels  42.7 us (98%)
  between operations  0.81 us (2%)
    pallas_call x1, Pallas kernels, local_step(): mid = step(g1, g2, w1, w2, m1, m2, v1, v2, tokens)  23.5 us
    pallas_call x1, Pallas kernels, local_step(): outs = tail(mid[0], targets, *mid[1:])  19.2 us

profile of v1, /device:TPU:0, one launch (start us, length us, event | category | flops | bytes accessed | tf_op | source)
XLA Modules:
  0.0 43.5 jit_solution(3041162356139342040)
XLA Ops:
  0.6 23.5 %step.1 = (bf16[8192,128]{1,0:T(8,128)(2,1)}, bf16[3,128,512]{2,1,0:T(8,128)(2,1)}, bf16[3,512,128]{2,1,0:T(8,128)(2,1)}, f32[3,32,512]{2,1,0:T(8,128)}, f32[3,1...) custom-call(f32[1,3,32,512]{3,2,1,0:T(8,128)} %refs_0_.1, ...), custom_call_target="tpu_custom_call" | custom-call | tf_op jit(solution)/shard_map/step/pallas_call | solution.py:251
  24.1 19.2 %tail.1 = (f32[1,8192]{1,0:T(1,128)}, bf16[3,128,512]{2,1,0:T(8,128)(2,1)}, bf16[3,512,128]{2,1,0:T(8,128)(2,1)}, f32[3,32,512]{2,1,0:T(8,128)}, f32[3,128,128]{...) custom-call(bf16[8192,128]{1,0:T(8,128)(2,1)} %get-tuple-element.27., ...), custom_call_target="tpu_custom_call" | custom-call | tf_op jit(solution)/shard_map/tail/pallas_call | solution.py:267

commit v2 on v0

v2 whole, which is shorter than its diff:
```python
import jax
import jax.numpy as jnp
from jax import lax
from jax.experimental import pallas as pl
from jax.experimental.pallas import tpu as pltpu
from jax.sharding import PartitionSpec as P

ADAM_BETA1 = 0.9
ADAM_BETA2 = 0.95
ADAM_EPS = 1e-8
WEIGHT_DECAY = 0.1
STEP = 2
NORM_EPS = 1e-6
LR_COEF = 0.2
GELU_A = 2.0 * (2.0 / jnp.pi) ** 0.5
GELU_B = 8.0 * (2.0 / jnp.pi) ** 0.5 * 0.044715

F32 = jnp.float32
BF16 = jnp.bfloat16
MESH = pl.DeviceIdType.MESH
ROWS = 2048
VMEM_LIMIT = 44 * 1024 * 1024


def adam_shard(grad_mean, master, moment1, moment2, learn_rate):
    new_m = ADAM_BETA1 * moment1 + (1.0 - ADAM_BETA1) * grad_mean
    new_v = ADAM_BETA2 * moment2 + (1.0 - ADAM_BETA2) * grad_mean * grad_mean
    corr_m = 1.0 - ADAM_BETA1 ** STEP
    corr_v = 1.0 - ADAM_BETA2 ** STEP
    step_dir = (new_m / corr_m) / (jnp.sqrt(new_v / corr_v) + ADAM_EPS)
    new_w = master - learn_rate * (step_dir + WEIGHT_DECAY * master)
    return new_w, new_m, new_v


def rms_norm(hidden):
    inv_rms = lax.rsqrt(jnp.mean(hidden * hidden, axis=-1, keepdims=True) + NORM_EPS)
    return (hidden * inv_rms).astype(BF16)


def mlp_up(normed, half_up):
    half = jnp.dot(normed.astype(F32), half_up, preferred_element_type=F32).astype(BF16).astype(F32)
    act = half * jnp.tanh(half * (GELU_B * (half * half) + GELU_A)) + half
    return act.astype(BF16)


def mlp_down(act, hidden, down):
    return (hidden + jnp.dot(act.astype(F32), down, preferred_element_type=F32)).astype(BF16)


def step_kernel(learn_rate, replicas,
                g1, g2, w1, w2, m1, m2, v1, v2, x,
                h_out, fw1, fw2, s1, s2,
                g1v, g2v, r1v, r2v, xv, nv, av, up, down,
                sem_g, sem_s, sem_x, send_g, recv_g, send_w, recv_w):
    rep, dat = lax.axis_index('replica'), lax.axis_index('data')
    layers = g1.shape[1]
    rows1, rows2 = w1.shape[1], w2.shape[1]
    tiles = x.shape[0] // ROWS
    sls = [pl.ds(t * ROWS, ROWS) for t in range(tiles)]
    twin = {'replica': 1 - rep}
    peers = [{'data': d} for d in (dat + 1 - 2 * lax.rem(dat, 2), lax.rem(dat + 2, 4), 3 - dat)]

    gcopies = [[pltpu.make_async_copy(g.at[0, l], gv.at[l], sem_g.at[l, k])
                for k, (g, gv) in enumerate(((g1, g1v), (g2, g2v)))] for l in range(layers)]
    for pair in gcopies:
        for c in pair:
            c.start()

    barrier = pltpu.get_barrier_semaphore()
    for dev in [twin] + peers:
        pl.semaphore_signal(barrier, inc=1, device_id=dev, device_id_type=MESH)
    with jax.named_scope('barrier'):
        pl.semaphore_wait(barrier, 4)

    half_cols = w1.shape[2] // 2
    pieces = [(0, 0, pl.ds(0, half_cols)), (0, 0, pl.ds(half_cols, half_cols)), (0, 1, slice(None))]
    pieces += [(l, k, slice(None)) for l in range(1, layers) for k in range(2)]
    gsends = []
    with jax.named_scope('gsend'):
        for p, (l, k, cols) in enumerate(pieces):
            gv, rv = ((g1v, r1v), (g2v, r2v))[k]
            if p != 1:
                gcopies[l][k].wait()
            c = pltpu.make_async_remote_copy(
                src_ref=gv.at[l, :, cols], dst_ref=rv.at[l, :, cols], send_sem=send_g.at[p], recv_sem=recv_g.at[p],
                device_id=twin, device_id_type=MESH)
            c.start()
            gsends.append(c)

    xcopies = [pltpu.make_async_copy(x.at[sl], xv.at[sl], sem_x.at[t]) for t, sl in enumerate(sls)]
    scopies = [pltpu.make_async_copy(src, dst.at[i], sem_s.at[k, i])
               for k, (srcs, dst) in enumerate((((w1, m1, v1), s1), ((w2, m2, v2), s2)))
               for i, src in enumerate(srcs)]
    for c in xcopies + scopies:
        c.start()
    for t, sl in enumerate(sls):
        with jax.named_scope('norm'):
            xcopies[t].wait()
            nv[sl] = rms_norm(xv[sl].astype(F32))
    for c in scopies:
        c.wait()

    wsends = []

    def update(p):
        l, k, cols = pieces[p]
        gv, rv, s, fw, rows = ((g1v, r1v, s1, fw1, rows1), (g2v, r2v, s2, fw2, rows2))[k]
        with jax.named_scope(f'waitg{p}'):
            gsends[p].wait_recv()
        mean = (gv[l, :, cols] + rv[l, :, cols]) / replicas
        new = adam_shard(mean, s[0, l, :, cols], s[1, l, :, cols], s[2, l, :, cols], learn_rate)
        for i in range(3):
            s[i, l, :, cols] = new[i]
        mine = pl.ds(pl.multiple_of(dat * rows, rows), rows)
        fw[l, mine, cols] = new[0].astype(BF16)
        out = []
        for j, dev in enumerate(peers):
            c = pltpu.make_async_remote_copy(
                src_ref=fw.at[l, mine, cols], dst_ref=fw.at[l, mine, cols], send_sem=send_w.at[p, j],
                recv_sem=recv_w.at[p, j], device_id=dev, device_id_type=MESH)
            c.start()
            out.append(c)
        wsends.append(out)

    def arrived(p):
        with jax.named_scope(f'waitw{p}'):
            for c in wsends[p]:
                c.wait_recv()

    def layer(l, ts):
        with jax.named_scope(f'layer{l}'):
            for t in ts:
                wide = xv[sls[t]].astype(F32)
                normed = nv[sls[t]] if l == 0 else rms_norm(wide)
                dst = h_out if l == 1 else xv
                dst[sls[t]] = mlp_down(mlp_up(normed, up[...]), wide, down[...])

    update(0)
    update(1)
    for p in range(2):
        arrived(p)
        cols = pieces[p][2]
        with jax.named_scope(f'up{p}'):
            up[:, cols] = fw1[0, :, cols].astype(F32) * 0.5
            av[sls[0], cols] = mlp_up(nv[sls[0]], up[:, cols])
        if p == 0:
            update(2)
    update(3)
    with jax.named_scope('up'):
        av[sls[1]] = mlp_up(nv[sls[1]], up[...])
    arrived(2)
    down[...] = fw2[0].astype(F32)
    update(4)
    with jax.named_scope('layer0'):
        for sl in sls[:2]:
            xv[sl] = mlp_down(av[sl], xv[sl].astype(F32), down[...])
        layer(0, range(2, tiles))
    update(5)
    update(6)
    arrived(3)
    arrived(4)
    up[...] = fw1[1].astype(F32) * 0.5
    down[...] = fw2[1].astype(F32)
    layer(1, range(tiles))
    arrived(5)
    arrived(6)
    with jax.named_scope('waitsend'):
        for c in gsends + [c for out in wsends for c in out]:
            c.wait_send()


def tail_kernel(h, fw1, fw2, s1, s2, y,
                loss, fw1_out, fw2_out, ow1, ow2, om1, om2, ov1, ov2,
                up, down, sem_f, sem_s):
    last = fw1.shape[0] - 1
    tiles = h.shape[0] // ROWS
    sls = [pl.ds(t * ROWS, ROWS) for t in range(tiles)]
    outs = [pltpu.make_async_copy(s.at[i], dst, sem_s.at[k, i])
            for k, (s, dsts) in enumerate(((s1, (ow1, om1, ov1)), (s2, (ow2, om2, ov2))))
            for i, dst in enumerate(dsts)]
    outs += [pltpu.make_async_copy(fw1, fw1_out, sem_f.at[0]), pltpu.make_async_copy(fw2, fw2_out, sem_f.at[1])]
    for c in outs:
        c.start()
    up[...] = fw1[last].astype(F32) * 0.5
    down[...] = fw2[last].astype(F32)
    with jax.named_scope('last'):
        for sl in sls:
            wide = h[sl].astype(F32)
            hidden = mlp_down(mlp_up(rms_norm(wide), up[...]), wide, down[...])
            diff = hidden.astype(F32) - y[sl].astype(F32)
            loss[:, sl] = jnp.mean(diff * diff, axis=-1, keepdims=True).reshape(1, ROWS)
    with jax.named_scope('waitout'):
        for c in outs:
            c.wait()


def solution(mesh):
    replicas = mesh.shape['replica']
    grad_spec = P('replica', None, 'data', None)
    shard_spec = P(None, 'data', None)
    row_spec = P(('replica', 'data'), None)
    loss_spec = P(('replica', 'data'))
    full_spec = P()

    def local_step(g1, g2, w1, w2, m1, m2, v1, v2, tokens, targets):
        learn_rate = LR_COEF * tokens.shape[1] ** -0.5
        n_rows, width = tokens.shape
        layers, rows1, hid = w1.shape
        rows2 = w2.shape[1]
        any_ = pl.BlockSpec(memory_space=pl.ANY)
        full1 = (layers, width, hid)
        full2 = (layers, hid, width)
        tiles = n_rows // ROWS
        pieces = 2 * layers + 1
        sh = jax.ShapeDtypeStruct
        dma = pltpu.SemaphoreType.DMA
        vmem = pl.BlockSpec(memory_space=pltpu.VMEM)
        step = pl.pallas_call(
            lambda *refs: step_kernel(learn_rate, replicas, *refs),
            out_shape=[pltpu.VMEM((n_rows, width), BF16), pltpu.VMEM(full1, BF16), pltpu.VMEM(full2, BF16),
                       pltpu.VMEM((3,) + w1.shape, F32), pltpu.VMEM((3,) + w2.shape, F32)],
            in_specs=[any_] * 9,
            out_specs=[vmem] * 5,
            scratch_shapes=[
                pltpu.VMEM(w1.shape, F32), pltpu.VMEM(w2.shape, F32),
                pltpu.VMEM(w1.shape, F32), pltpu.VMEM(w2.shape, F32),
                pltpu.VMEM((n_rows, width), BF16), pltpu.VMEM((n_rows, width), BF16),
                pltpu.VMEM((2 * ROWS, hid), BF16),
                pltpu.VMEM((width, hid), F32), pltpu.VMEM((hid, width), F32),
                dma((layers, 2)), dma((2, 3)), dma((tiles,)),
                dma((pieces,)), dma((pieces,)), dma((pieces, 3)), dma((pieces, 3)),
            ],
            compiler_params=pltpu.CompilerParams(
                collective_id=0, has_side_effects=True, vmem_limit_bytes=VMEM_LIMIT),
            name='step',
        )
        mid = step(*(pltpu.with_memory_space_constraint(a, pltpu.HBM)
                     for a in (g1, g2, w1, w2, m1, m2, v1, v2, tokens)))
        mid = [pltpu.with_memory_space_constraint(a, pltpu.VMEM) for a in mid]
        tail = pl.pallas_call(
            tail_kernel,
            out_shape=[sh((1, n_rows), F32), sh(full1, BF16), sh(full2, BF16)]
            + [sh(w1.shape, F32), sh(w2.shape, F32)] * 3,
            in_specs=[vmem] * 6,
            out_specs=[vmem] + [any_] * 8,
            scratch_shapes=[
                pltpu.VMEM((width, hid), F32), pltpu.VMEM((hid, width), F32),
                dma((2,)), dma((2, 3)),
            ],
            compiler_params=pltpu.CompilerParams(vmem_limit_bytes=VMEM_LIMIT),
            name='tail',
        )
        outs = tail(*mid, targets)
        return (outs[0].reshape(n_rows),) + tuple(outs[1:])

    return jax.shard_map(
        local_step,
        mesh=mesh,
        in_specs=(grad_spec, grad_spec, shard_spec, shard_spec, shard_spec, shard_spec, shard_spec, shard_spec, row_spec, row_spec),
        out_specs=(loss_spec, full_spec, full_spec, shard_spec, shard_spec, shard_spec, shard_spec, shard_spec, shard_spec),
        check_vma=False,
    )
```

time: 124 us -> 35.3 us (0.28)
  blocking collectives: 47.9 us -> 0 us
  Pallas kernels: 0 us -> 34.4 us
  matrix products: 29.9 us -> 0 us
  waiting for transfers between devices: 18.3 us -> 0 us
  between operations: 14.2 us -> 0.83 us
  local copies, waits for them, and re-layouts: 7.16 us -> 0.01 us
  other arithmetic: 6.36 us -> 0 us
    all_gather x6 -> x0, blocking collectives: 47.9 us -> none  [the longest x3 25.2 us: local_step(): layer_w1 = lax.all_gather(half_w1[layer_idx], 'data', axis=0, tiled=True)]
    pallas_call x0 -> x2, Pallas kernels: none -> 34.4 us  [the longest x1 26.3 us: local_step(): step(*(pltpu.with_memory_space_constraint(a, pltpu.HBM) for a in (g1, g2,...]
    dot_general x3 -> x0, matrix products: 29.9 us -> none  [block_forward(): down_out = jnp.dot(gelu_act, w_down, preferred_element_type=jnp.float32)]
    psum x1 -> x0, waiting for transfers between devices: 17.6 us -> none  [local_step(): grad_mean2 = lax.psum(grad_w2[0], 'replica') / replicas]
    unnamed x16 -> x2, local copies, waits for them, and re-layouts: 7.14 us -> 0.01 us
    convert_element_type x2 -> x0, other arithmetic: 3.66 us -> none  [the longest x1 1.83 us: local_step(): half_w2 = new_w2.astype(jnp.bfloat16)]
    another operation x2 -> x0, other arithmetic: 1.58 us -> none  [the longest x1 0.79 us: local_step(): jnp.stack(gathered_w1)]
  transfers between devices with their start and end apart: 1 -> 0, of which waited for: 1 -> 0; matrix products, arithmetic and copies ran while one was open for 6% -> 0% of each run, Pallas kernels for 0% -> 0%
where the time goes in v2:
time: 35.3 us; the launch traced here: 35.2 us
  Pallas kernels  34.4 us (97%)
  between operations  0.83 us (2%)
    pallas_call x1, Pallas kernels, local_step(): step(*(pltpu.with_memory_space_constraint(a, pltpu.HBM) for a in (g1, g2,...  26.3 us
    pallas_call x1, Pallas kernels, local_step(): outs = tail(*mid, targets)  8.09 us

profile of v2, /device:TPU:0, one launch (start us, length us, event | category | flops | bytes accessed | tf_op | source)
XLA Modules:
  0.0 35.2 jit_solution(13281473132109239510)
XLA Ops:
  0.6 0.0 copy-start
  0.7 26.3 %step.1 = (bf16[8192,128]{1,0:T(8,128)(2,1)S(1)}, bf16[3,128,512]{2,1,0:T(8,128)(2,1)S(1)}, bf16[3,512,128]{2,1,0:T(8,128)(2,1)S(1)}, f32[3,3,32,512]{3,2,1,0:T(8,128)S(1)}, f32[3,3,128,128]{3,2,1,0:T(8,128)S(1)}) custom-call(f32[1,3,32,512]{3,2,1,0:T(8,128)} %refs_0_.1, f32[1,3,128,128]{3,2,1,0:T(8,128)} %refs_1_.1, f32[3,32,512]{2,1,0:T(8,128)} %refs_2_.1, ...), custom_call_target="tpu_custom_call" | custom-call | tf_op jit(solution)/shard_map/step/pallas_call | solution.py:237
  26.9 0.0 copy-done
  27.0 8.1 %tail.1 = (f32[1,8192]{1,0:T(1,128)}, bf16[3,128,512]{2,1,0:T(8,128)(2,1)}, bf16[3,512,128]{2,1,0:T(8,128)(2,1)}, f32[3,32,512]{2,1,0:T(8,128)}, f32[3,128,128]{...) custom-call(bf16[8192,128]{1,0:T(8,128)(2,1)S(1)} %get-tuple-element, ...), custom_call_target="tpu_custom_call" | custom-call | tf_op jit(solution)/shard_map/tail/pallas_call | solution.py:253
Async XLA Ops:
  0.6 26.3 %copy-start = (bf16[8192,128]{1,0:T(8,128)(2,1)S(1)}, bf16[8192,128]{1,0:T(8,128)(2,1)}, u32[]{:S(2)}) copy-start(bf16[8192,128]{1,0:T(8,128)(2,1)} %y.1) | copy-start | bytes 6291460

commit v3 on v2

--- a/solution.py
+++ b/solution.py
@@ -19,6 +19,10 @@
 BF16 = jnp.bfloat16
 MESH = pl.DeviceIdType.MESH
 ROWS = 2048
+PIECE_ROWS = 4096
+EARLY_ROWS = 4096
+MID_ROWS = 6144
+CUTS = 4
 VMEM_LIMIT = 44 * 1024 * 1024
 
 
@@ -37,19 +41,27 @@
     return (hidden * inv_rms).astype(BF16)
 
 
+def row_mean_sq(rows):
+    return jnp.sum((rows * rows).T, axis=0, keepdims=True) * (1.0 / rows.shape[1])
+
+
+def rms_norm_t(hidden):
+    inv_rms = lax.rsqrt(row_mean_sq(hidden) + NORM_EPS)
+    return (hidden * jnp.broadcast_to(inv_rms, hidden.shape[::-1]).T).astype(BF16)
+
+
 def mlp_up(normed, half_up):
-    half = jnp.dot(normed.astype(F32), half_up, preferred_element_type=F32).astype(BF16).astype(F32)
-    act = half * jnp.tanh(half * (GELU_B * (half * half) + GELU_A)) + half
-    return act.astype(BF16)
+    half = jnp.dot(normed, half_up, preferred_element_type=F32).astype(BF16).astype(F32)
+    return half * jnp.tanh(half * (GELU_B * (half * half) + GELU_A)) + half
 
 
 def mlp_down(act, hidden, down):
-    return (hidden + jnp.dot(act.astype(F32), down, preferred_element_type=F32)).astype(BF16)
+    return (hidden + jnp.dot(act, down, preferred_element_type=F32)).astype(BF16)
 
 
 def step_kernel(learn_rate, replicas,
                 g1, g2, w1, w2, m1, m2, v1, v2, x,
-                h_out, fw1, fw2, s1, s2,
+                h_out, n_out, fw1, fw2, s1, s2,
                 g1v, g2v, r1v, r2v, xv, nv, av, up, down,
                 sem_g, sem_s, sem_x, send_g, recv_g, send_w, recv_w):
     rep, dat = lax.axis_index('replica'), lax.axis_index('data')
@@ -72,14 +84,14 @@
     with jax.named_scope('barrier'):
         pl.semaphore_wait(barrier, 4)
 
-    half_cols = w1.shape[2] // 2
-    pieces = [(0, 0, pl.ds(0, half_cols)), (0, 0, pl.ds(half_cols, half_cols)), (0, 1, slice(None))]
+    cut = w1.shape[2] // CUTS
+    pieces = [(0, 0, pl.ds(i * cut, cut)) for i in range(CUTS)] + [(0, 1, slice(None))]
     pieces += [(l, k, slice(None)) for l in range(1, layers) for k in range(2)]
     gsends = []
     with jax.named_scope('gsend'):
         for p, (l, k, cols) in enumerate(pieces):
             gv, rv = ((g1v, r1v), (g2v, r2v))[k]
-            if p != 1:
+            if p not in range(1, CUTS):
                 gcopies[l][k].wait()
             c = pltpu.make_async_remote_copy(
                 src_ref=gv.at[l, :, cols], dst_ref=rv.at[l, :, cols], send_sem=send_g.at[p], recv_sem=recv_g.at[p],
@@ -127,68 +139,70 @@
             for c in wsends[p]:
                 c.wait_recv()
 
-    def layer(l, ts):
-        with jax.named_scope(f'layer{l}'):
-            for t in ts:
-                wide = xv[sls[t]].astype(F32)
-                normed = nv[sls[t]] if l == 0 else rms_norm(wide)
-                dst = h_out if l == 1 else xv
-                dst[sls[t]] = mlp_down(mlp_up(normed, up[...]), wide, down[...])
-
-    update(0)
-    update(1)
-    for p in range(2):
+    n_rows = x.shape[0]
+
+    def finish(sl, act, h_ref, n_ref):
+        hidden = mlp_down(act, xv[sl].astype(F32), down[...])
+        h_ref[sl] = hidden
+        n_ref[sl] = rms_norm_t(hidden.astype(F32))
+
+    for p in range(CUTS + 1):
+        update(p)
+    early = pl.ds(0, PIECE_ROWS)
+    for p in range(CUTS):
         arrived(p)
         cols = pieces[p][2]
         with jax.named_scope(f'up{p}'):
-            up[:, cols] = fw1[0, :, cols].astype(F32) * 0.5
-            av[sls[0], cols] = mlp_up(nv[sls[0]], up[:, cols])
-        if p == 0:
-            update(2)
-    update(3)
-    with jax.named_scope('up'):
-        av[sls[1]] = mlp_up(nv[sls[1]], up[...])
-    arrived(2)
+            up[:, cols] = fw1[0, :, cols] * 0.5
+            av[early, cols] = mlp_up(nv[early], up[:, cols])
+        if p == 1:
+            update(CUTS + 1)
+    if EARLY_ROWS > PIECE_ROWS:
+        with jax.named_scope('up'):
+            sl = pl.ds(PIECE_ROWS, EARLY_ROWS - PIECE_ROWS)
+            av[sl] = mlp_up(nv[sl], up[...])
+    arrived(CUTS)
     down[...] = fw2[0].astype(F32)
-    update(4)
+    update(CUTS + 2)
     with jax.named_scope('layer0'):
-        for sl in sls[:2]:
-            xv[sl] = mlp_down(av[sl], xv[sl].astype(F32), down[...])
-        layer(0, range(2, tiles))
-    update(5)
-    update(6)
-    arrived(3)
-    arrived(4)
-    up[...] = fw1[1].astype(F32) * 0.5
-    down[...] = fw2[1].astype(F32)
-    layer(1, range(tiles))
-    arrived(5)
-    arrived(6)
+        sl = pl.ds(0, EARLY_ROWS)
+        finish(sl, av[sl], xv, nv)
+        sl = pl.ds(EARLY_ROWS, MID_ROWS - EARLY_ROWS)
+        finish(sl, mlp_up(nv[sl], up[...]), xv, nv)
+    update(CUTS + 3)
+    update(CUTS + 4)
+    arrived(CUTS + 1)
+    arrived(CUTS + 2)
+    with jax.named_scope('layer1'):
+        if n_rows > MID_ROWS:
+            sl = pl.ds(MID_ROWS, n_rows - MID_ROWS)
+            finish(sl, mlp_up(nv[sl], up[...]), xv, nv)
+        up[...] = fw1[1] * 0.5
+        down[...] = fw2[1].astype(F32)
+        sl = pl.ds(0, n_rows)
+        finish(sl, mlp_up(nv[sl], up[...]), h_out, n_out)
+    arrived(CUTS + 3)
+    arrived(CUTS + 4)
     with jax.named_scope('waitsend'):
         for c in gsends + [c for out in wsends for c in out]:
             c.wait_send()
 
 
-def tail_kernel(h, fw1, fw2, s1, s2, y,
+def tail_kernel(h, n, fw1, fw2, s1, s2, y,
                 loss, fw1_out, fw2_out, ow1, ow2, om1, om2, ov1, ov2,
                 up, down, sem_f, sem_s):
     last = fw1.shape[0] - 1
-    tiles = h.shape[0] // ROWS
-    sls = [pl.ds(t * ROWS, ROWS) for t in range(tiles)]
     outs = [pltpu.make_async_copy(s.at[i], dst, sem_s.at[k, i])
             for k, (s, dsts) in enumerate(((s1, (ow1, om1, ov1)), (s2, (ow2, om2, ov2))))
             for i, dst in enumerate(dsts)]
     outs += [pltpu.make_async_copy(fw1, fw1_out, sem_f.at[0]), pltpu.make_async_copy(fw2, fw2_out, sem_f.at[1])]
     for c in outs:
         c.start()
-    up[...] = fw1[last].astype(F32) * 0.5
-    down[...] = fw2[last].astype(F32)
     with jax.named_scope('last'):
-        for sl in sls:
-            wide = h[sl].astype(F32)
-            hidden = mlp_down(mlp_up(rms_norm(wide), up[...]), wide, down[...])
-            diff = hidden.astype(F32) - y[sl].astype(F32)
-            loss[:, sl] = jnp.mean(diff * diff, axis=-1, keepdims=True).reshape(1, ROWS)
+        up[...] = fw1[last] * 0.5
+        down[...] = fw2[last].astype(F32)
+        hidden = mlp_down(mlp_up(n[...], up[...]), h[...].astype(F32), down[...])
+        loss[...] = row_mean_sq(hidden.astype(F32) - y[...].astype(F32))
     with jax.named_scope('waitout'):
         for c in outs:
             c.wait()
@@ -211,22 +225,22 @@
         full1 = (layers, width, hid)
         full2 = (layers, hid, width)
         tiles = n_rows // ROWS
-        pieces = 2 * layers + 1
+        pieces = 2 * layers - 1 + CUTS
         sh = jax.ShapeDtypeStruct
         dma = pltpu.SemaphoreType.DMA
         vmem = pl.BlockSpec(memory_space=pltpu.VMEM)
         step = pl.pallas_call(
             lambda *refs: step_kernel(learn_rate, replicas, *refs),
-            out_shape=[pltpu.VMEM((n_rows, width), BF16), pltpu.VMEM(full1, BF16), pltpu.VMEM(full2, BF16),
+            out_shape=[pltpu.VMEM((n_rows, width), BF16), pltpu.VMEM((n_rows, width), BF16), pltpu.VMEM(full1, BF16), pltpu.VMEM(full2, BF16),
                        pltpu.VMEM((3,) + w1.shape, F32), pltpu.VMEM((3,) + w2.shape, F32)],
             in_specs=[any_] * 9,
-            out_specs=[vmem] * 5,
+            out_specs=[vmem] * 6,
             scratch_shapes=[
                 pltpu.VMEM(w1.shape, F32), pltpu.VMEM(w2.shape, F32),
                 pltpu.VMEM(w1.shape, F32), pltpu.VMEM(w2.shape, F32),
                 pltpu.VMEM((n_rows, width), BF16), pltpu.VMEM((n_rows, width), BF16),
-                pltpu.VMEM((2 * ROWS, hid), BF16),
-                pltpu.VMEM((width, hid), F32), pltpu.VMEM((hid, width), F32),
+                pltpu.VMEM((EARLY_ROWS, hid), F32),
+                pltpu.VMEM((width, hid), BF16), pltpu.VMEM((hid, width), F32),
                 dma((layers, 2)), dma((2, 3)), dma((tiles,)),
                 dma((pieces,)), dma((pieces,)), dma((pieces, 3)), dma((pieces, 3)),
             ],
@@ -241,10 +255,10 @@
             tail_kernel,
             out_shape=[sh((1, n_rows), F32), sh(full1, BF16), sh(full2, BF16)]
             + [sh(w1.shape, F32), sh(w2.shape, F32)] * 3,
-            in_specs=[vmem] * 6,
+            in_specs=[vmem] * 7,
             out_specs=[vmem] + [any_] * 8,
             scratch_shapes=[
-                pltpu.VMEM((width, hid), F32), pltpu.VMEM((hid, width), F32),
+                pltpu.VMEM((width, hid), BF16), pltpu.VMEM((hid, width), F32),
                 dma((2,)), dma((2, 3)),
             ],
             compiler_params=pltpu.CompilerParams(vmem_limit_bytes=VMEM_LIMIT),

time: 35.3 us -> 33.1 us (0.938)
  Pallas kernels: 34.4 us -> 32.1 us
    pallas_call x1, Pallas kernels: 26.3 us -> 25.1 us  [local_step(): step(*(pltpu.with_memory_space_constraint(a, pltpu.HBM) for a in (g1, g2,...]
    pallas_call x1, Pallas kernels: 8.09 us -> 7 us  [local_step(): outs = tail(*mid, targets)]
where the time goes in v3:
time: 33.1 us; the launch traced here: 33 us
  Pallas kernels  32.1 us (97%)
  between operations  0.83 us (3%)
    pallas_call x1, Pallas kernels, local_step(): step(*(pltpu.with_memory_space_constraint(a, pltpu.HBM) for a in (g1, g2,...  25.1 us
    pallas_call x1, Pallas kernels, local_step(): outs = tail(*mid, targets)  7 us

profile of v3, /device:TPU:0, one launch (start us, length us, event | category | flops | bytes accessed | tf_op | source)
XLA Modules:
  0.0 33.0 jit_solution(2908239436904822358)
XLA Ops:
  0.6 0.0 copy-start
  0.7 25.1 %step.1 = (bf16[8192,128]{1,0:T(8,128)(2,1)S(1)}, bf16[8192,128]{1,0:T(8,128)(2,1)S(1)}, bf16[3,128,512]{2,1,0:T(8,128)(2,1)S(1)}, bf16[3,512,128]{2,1,0:T(8,128...) custom-call(f32[1,3,32,512]{3,2,1,0:T(8,128)} %refs_0_.1, f32[1,3,128,128]{3,2,1,0:T(8,128)} %refs_1_.1, ...), custom_call_target="tpu_custom_call" | custom-call | tf_op jit(solution)/shard_map/step/pallas_call | solution.py:251
  25.8 0.0 copy-done
  25.8 7.0 %tail.1 = (f32[1,8192]{1,0:T(1,128)}, bf16[3,128,512]{2,1,0:T(8,128)(2,1)}, bf16[3,512,128]{2,1,0:T(8,128)(2,1)}, f32[3,32,512]{2,1,0:T(8,128)}, f32[3,128,128]{...) custom-call(bf16[8192,128]{1,0:T(8,128)(2,1)S(1)} %get-tuple-element, ...), custom_call_target="tpu_custom_call" | custom-call | tf_op jit(solution)/shard_map/tail/pallas_call | solution.py:267
Async XLA Ops:
  0.6 25.2 %copy-start = (bf16[8192,128]{1,0:T(8,128)(2,1)S(1)}, bf16[8192,128]{1,0:T(8,128)(2,1)}, u32[]{:S(2)}) copy-start(bf16[8192,128]{1,0:T(8,128)(2,1)} %y.1) | copy-start | bytes 6291460

commit v4 on v3

--- a/solution.py
+++ b/solution.py
@@ -46,8 +46,9 @@
 
 
 def rms_norm_t(hidden):
-    inv_rms = lax.rsqrt(row_mean_sq(hidden) + NORM_EPS)
-    return (hidden * jnp.broadcast_to(inv_rms, hidden.shape[::-1]).T).astype(BF16)
+    cols = hidden.T.astype(F32)
+    inv_rms = lax.rsqrt(jnp.sum(cols * cols, axis=0, keepdims=True) * (1.0 / cols.shape[0]) + NORM_EPS)
+    return (cols * inv_rms).astype(BF16).T
 
 
 def mlp_up(normed, half_up):
@@ -57,6 +58,10 @@
 
 def mlp_down(act, hidden, down):
     return (hidden + jnp.dot(act, down, preferred_element_type=F32)).astype(BF16)
+
+
+def wait_bytes(ref, sem):
+    pltpu.make_async_copy(ref, ref, sem).wait()
 
 
 def step_kernel(learn_rate, replicas,
@@ -72,11 +77,11 @@
     twin = {'replica': 1 - rep}
     peers = [{'data': d} for d in (dat + 1 - 2 * lax.rem(dat, 2), lax.rem(dat + 2, 4), 3 - dat)]
 
-    gcopies = [[pltpu.make_async_copy(g.at[0, l], gv.at[l], sem_g.at[l, k])
-                for k, (g, gv) in enumerate(((g1, g1v), (g2, g2v)))] for l in range(layers)]
-    for pair in gcopies:
-        for c in pair:
-            c.start()
+    gcopies = [pltpu.make_async_copy(g1.at[0, 0], g1v.at[0], sem_g.at[0]),
+               pltpu.make_async_copy(g2.at[0], g2v, sem_g.at[1]),
+               pltpu.make_async_copy(g1.at[0, pl.ds(1, layers - 1)], g1v.at[pl.ds(1, layers - 1)], sem_g.at[2])]
+    for c in gcopies:
+        c.start()
 
     barrier = pltpu.get_barrier_semaphore()
     for dev in [twin] + peers:
@@ -91,28 +96,27 @@
     with jax.named_scope('gsend'):
         for p, (l, k, cols) in enumerate(pieces):
             gv, rv = ((g1v, r1v), (g2v, r2v))[k]
-            if p not in range(1, CUTS):
-                gcopies[l][k].wait()
+            if p in (0, CUTS, CUTS + 1):
+                gcopies[(0, CUTS, CUTS + 1).index(p)].wait()
             c = pltpu.make_async_remote_copy(
-                src_ref=gv.at[l, :, cols], dst_ref=rv.at[l, :, cols], send_sem=send_g.at[p], recv_sem=recv_g.at[p],
+                src_ref=gv.at[l, :, cols], dst_ref=rv.at[l, :, cols], send_sem=send_g, recv_sem=recv_g.at[p],
                 device_id=twin, device_id_type=MESH)
             c.start()
             gsends.append(c)
 
-    xcopies = [pltpu.make_async_copy(x.at[sl], xv.at[sl], sem_x.at[t]) for t, sl in enumerate(sls)]
-    scopies = [pltpu.make_async_copy(src, dst.at[i], sem_s.at[k, i])
-               for k, (srcs, dst) in enumerate((((w1, m1, v1), s1), ((w2, m2, v2), s2)))
-               for i, src in enumerate(srcs)]
+    mid = x.shape[0] // 2
+    xcopies = [pltpu.make_async_copy(x.at[sl], xv.at[sl], sem_x.at[t]) for t, sl in enumerate((pl.ds(0, mid), pl.ds(mid, mid)))]
+    scopies = [pltpu.make_async_copy(src, dst.at[i], sem_s)
+               for srcs, dst in (((w1, m1, v1), s1), ((w2, m2, v2), s2)) for i, src in enumerate(srcs)]
     for c in xcopies + scopies:
         c.start()
     for t, sl in enumerate(sls):
         with jax.named_scope('norm'):
-            xcopies[t].wait()
+            if t % (tiles // 2) == 0:
+                xcopies[t // (tiles // 2)].wait()
             nv[sl] = rms_norm(xv[sl].astype(F32))
-    for c in scopies:
-        c.wait()
-
-    wsends = []
+    row_bytes = av.shape[1] * 4
+    wait_bytes(av.at[pl.ds(0, 3 * (w1.size + w2.size) * 4 // row_bytes)], sem_s)
 
     def update(p):
         l, k, cols = pieces[p]
@@ -125,26 +129,23 @@
             s[i, l, :, cols] = new[i]
         mine = pl.ds(pl.multiple_of(dat * rows, rows), rows)
         fw[l, mine, cols] = new[0].astype(BF16)
-        out = []
-        for j, dev in enumerate(peers):
-            c = pltpu.make_async_remote_copy(
-                src_ref=fw.at[l, mine, cols], dst_ref=fw.at[l, mine, cols], send_sem=send_w.at[p, j],
-                recv_sem=recv_w.at[p, j], device_id=dev, device_id_type=MESH)
-            c.start()
-            out.append(c)
-        wsends.append(out)
+        for dev in peers:
+            pltpu.make_async_remote_copy(
+                src_ref=fw.at[l, mine, cols], dst_ref=fw.at[l, mine, cols], send_sem=send_w,
+                recv_sem=recv_w.at[p], device_id=dev, device_id_type=MESH).start()
 
     def arrived(p):
+        l, k, cols = pieces[p]
+        fw, rows = ((fw1, rows1), (fw2, rows2))[k]
         with jax.named_scope(f'waitw{p}'):
-            for c in wsends[p]:
-                c.wait_recv()
+            wait_bytes(fw.at[l, pl.ds(0, len(peers) * rows), cols], recv_w.at[p])
 
     n_rows = x.shape[0]
 
     def finish(sl, act, h_ref, n_ref):
         hidden = mlp_down(act, xv[sl].astype(F32), down[...])
         h_ref[sl] = hidden
-        n_ref[sl] = rms_norm_t(hidden.astype(F32))
+        n_ref[sl] = rms_norm(hidden.astype(F32))
 
     for p in range(CUTS + 1):
         update(p)
@@ -184,18 +185,17 @@
     arrived(CUTS + 3)
     arrived(CUTS + 4)
     with jax.named_scope('waitsend'):
-        for c in gsends + [c for out in wsends for c in out]:
-            c.wait_send()
+        wait_bytes(av.at[pl.ds(0, (w1.size + w2.size) * 4 // row_bytes)], send_g)
+        wait_bytes(av.at[pl.ds(0, len(peers) * (w1.size + w2.size) * 2 // row_bytes)], send_w)
 
 
 def tail_kernel(h, n, fw1, fw2, s1, s2, y,
                 loss, fw1_out, fw2_out, ow1, ow2, om1, om2, ov1, ov2,
-                up, down, sem_f, sem_s):
+                up, down, sem):
     last = fw1.shape[0] - 1
-    outs = [pltpu.make_async_copy(s.at[i], dst, sem_s.at[k, i])
-            for k, (s, dsts) in enumerate(((s1, (ow1, om1, ov1)), (s2, (ow2, om2, ov2))))
-            for i, dst in enumerate(dsts)]
-    outs += [pltpu.make_async_copy(fw1, fw1_out, sem_f.at[0]), pltpu.make_async_copy(fw2, fw2_out, sem_f.at[1])]
+    outs = [pltpu.make_async_copy(s.at[i], dst, sem)
+            for s, dsts in ((s1, (ow1, om1, ov1)), (s2, (ow2, om2, ov2))) for i, dst in enumerate(dsts)]
+    outs += [pltpu.make_async_copy(fw1, fw1_out, sem), pltpu.make_async_copy(fw2, fw2_out, sem)]
     for c in outs:
         c.start()
     with jax.named_scope('last'):
@@ -204,8 +204,8 @@
         hidden = mlp_down(mlp_up(n[...], up[...]), h[...].astype(F32), down[...])
         loss[...] = row_mean_sq(hidden.astype(F32) - y[...].astype(F32))
     with jax.named_scope('waitout'):
-        for c in outs:
-            c.wait()
+        moved = (s1.size + s2.size) * 4 + (fw1.size + fw2.size) * 2
+        wait_bytes(h.at[pl.ds(0, moved // (h.shape[1] * 2))], sem)
 
 
 def solution(mesh):
@@ -241,8 +241,8 @@
                 pltpu.VMEM((n_rows, width), BF16), pltpu.VMEM((n_rows, width), BF16),
                 pltpu.VMEM((EARLY_ROWS, hid), F32),
                 pltpu.VMEM((width, hid), BF16), pltpu.VMEM((hid, width), F32),
-                dma((layers, 2)), dma((2, 3)), dma((tiles,)),
-                dma((pieces,)), dma((pieces,)), dma((pieces, 3)), dma((pieces, 3)),
+                dma((3,)), dma, dma((2,)),
+                dma, dma((pieces,)), dma, dma((pieces,)),
             ],
             compiler_params=pltpu.CompilerParams(
                 collective_id=0, has_side_effects=True, vmem_limit_bytes=VMEM_LIMIT),
@@ -259,7 +259,7 @@
             out_specs=[vmem] + [any_] * 8,
             scratch_shapes=[
                 pltpu.VMEM((width, hid), BF16), pltpu.VMEM((hid, width), F32),
-                dma((2,)), dma((2, 3)),
+                dma,
             ],
             compiler_params=pltpu.CompilerParams(vmem_limit_bytes=VMEM_LIMIT),
             name='tail',

time: 33.1 us -> 32 us (0.967)
  Pallas kernels: 32.1 us -> 31.1 us
    pallas_call x1, Pallas kernels: 25.1 us -> 24.2 us  [local_step(): step(*(pltpu.with_memory_space_constraint(a, pltpu.HBM) for a in (g1, g2,...]
where the time goes in v4:
time: 32 us; the launch traced here: 31.9 us
  Pallas kernels  31.1 us (97%)
  between operations  0.83 us (3%)
    pallas_call x1, Pallas kernels, local_step(): step(*(pltpu.with_memory_space_constraint(a, pltpu.HBM) for a in (g1, g2,...  24.2 us
    pallas_call x1, Pallas kernels, local_step(): outs = tail(*mid, targets)  6.93 us

profile of v4, /device:TPU:0, one launch (start us, length us, event | category | flops | bytes accessed | tf_op | source)
XLA Modules:
  0.0 31.9 jit_solution(10149248868252661439)
XLA Ops:
  0.6 0.0 copy-start
  0.7 24.2 %step.1 = (bf16[8192,128]{1,0:T(8,128)(2,1)S(1)}, bf16[8192,128]{1,0:T(8,128)(2,1)S(1)}, bf16[3,128,512]{2,1,0:T(8,128)(2,1)S(1)}, bf16[3,512,128]{2,1,0:T(8,128...) custom-call(f32[1,3,32,512]{3,2,1,0:T(8,128)} %refs_0_.1, f32[1,3,128,128]{3,2,1,0:T(8,128)} %refs_1_.1, ...), custom_call_target="tpu_custom_call" | custom-call | tf_op jit(solution)/shard_map/step/pallas_call | solution.py:251
  24.8 0.0 copy-done
  24.8 6.9 %tail.1 = (f32[1,8192]{1,0:T(1,128)}, bf16[3,128,512]{2,1,0:T(8,128)(2,1)}, bf16[3,512,128]{2,1,0:T(8,128)(2,1)}, f32[3,32,512]{2,1,0:T(8,128)}, f32[3,128,128]{...) custom-call(bf16[8192,128]{1,0:T(8,128)(2,1)S(1)} %get-tuple-element, ...), custom_call_target="tpu_custom_call" | custom-call | tf_op jit(solution)/shard_map/tail/pallas_call | solution.py:267
Async XLA Ops:
  0.6 24.2 %copy-start = (bf16[8192,128]{1,0:T(8,128)(2,1)S(1)}, bf16[8192,128]{1,0:T(8,128)(2,1)}, u32[]{:S(2)}) copy-start(bf16[8192,128]{1,0:T(8,128)(2,1)} %y.1) | copy-start | bytes 6291460
